TPU v7x, 32 devices: a whole 2x2x4 slice. The times are simulated.
32 devices in a mesh: mem: 2 (over y), lat: 4 (over z), lon: 4 (over x, core).
Axes of the slice: x: 2, y: 2, z: 4, core: 2. Of those that a mesh axis runs over, the one named last changes fastest.
Arguments:
- control: bfloat16 [62, 3, 4, 4, 73728], P('mem', None, 'lat', 'lon'), may hold values from -6 to 6
- perturbs: bfloat16 [62, 3, 4, 4, 73728], P('mem', None, 'lat', 'lon'), may hold values from -0.75 to 0.75
- static_input: bfloat16 [3, 4, 4, 73728], P(None, 'lat', 'lon'), may hold values from -6 to 6
- lat_basis: bfloat16 [768, 384], replicated, may hold values from -0.21875 to 0.21875
- local_spectrum: float32 [384, 768], P(None, 'lat'), may hold values from 0.1 to 1
- static_spectrum: float32 [384, 768], P(None, 'lat'), may hold values from 0.1 to 1
- static_weight: float32 [3], replicated, may hold values from 0.2 to 0.8
Outputs:
- increment: float32 [3, 4, 4, 73728], P(None, 'lat', 'lon')
All inputs are finite; a program needn't handle non-finite values.
Results may differ from a plain program's by a relative error of at most 0.0073.
Values may be sent and summed in bfloat16 or wider, within the bound.
A program may use at most 128 MiB of HBM per device.

v0:
```python
import functools

import jax
import jax.numpy as jnp
import numpy as np
from jax import lax
from jax.experimental import pallas as pl
from jax.experimental.pallas import tpu as pltpu
from jax.sharding import PartitionSpec as P

NLON = 1536
NLAT = 768
KLON = 768
LANES = 128
HALF = 64
GROUP = 8
STEP_ROWS = 32
AHEAD = 4
MESH = pl.DeviceIdType.MESH
F32, BF16 = jnp.float32, jnp.bfloat16


def zonal_table():
    half = KLON // 2
    column = np.arange(KLON)
    wave = np.where(column < half, column, column - half + 1)
    angle = 2.0 * np.pi / NLON * (np.arange(NLON)[:, None] * wave[None, :] % NLON)
    values = np.where(column[None, :] < half, np.cos(angle), np.sin(angle))
    return (np.sqrt(2.0 / NLON) * values).astype(jnp.bfloat16)


def packed_table(n_lat):
    blocks = zonal_table().reshape(NLON, n_lat, KLON // n_lat)
    main = blocks[:, :, :LANES].reshape(NLON, -1)
    rest = blocks[:, :, LANES:]
    swapped = rest.reshape(NLON, n_lat // 2, 2, HALF)[:, :, ::-1]
    return np.concatenate([main, rest.reshape(NLON, -1), swapped.reshape(NLON, -1)], 1)


def aligned(start, to):
    return pl.multiple_of(start, to)


def kernel(
    sizes,
    ctrl, ctrl_last, pert, pert_last, table_in, merid_in, merid_t_in, spec_in, weight,
    out,
    xin, wst, zin, bin_, gin, table, merid, merid_t, spec,
    scaled, rows_in, waves, rows_out, grid, pbuf, part, peer,
    csem, xs, xr, zs, zr, bs, br, gs, gr, ms, mr, ps,
):
    levels, n_lat, n_lon, rows, cols, step = sizes
    blocks = rows // step
    chunks = levels * blocks
    width = step * cols
    pair = 3 * LANES
    pairs = GROUP // 2
    rest_a = n_lat * LANES
    rest_b = rest_a + n_lat * HALF
    my_mem, my_lat, my_lon = lax.axis_index("mem"), lax.axis_index("lat"), lax.axis_index("lon")
    lon_order = [2, 3, 1] if n_lon == 4 else list(range(1, n_lon))
    lat_order = [2, 3, 1] if n_lat == 4 else list(range(1, n_lat))

    def at_lon(lon):
        return (my_mem, my_lat, lon)

    def at_lat(lat):
        return (my_mem, lat, my_lon)

    def split(c):
        return lax.div(c, blocks), lax.rem(c, blocks)

    def cells(b):
        return pl.ds(aligned(b * width, LANES), width)

    def band(b):
        return pl.ds(aligned(b * step, 16), step)

    def remote(src, dst, send, recv, device):
        pltpu.make_async_remote_copy(
            src_ref=src, dst_ref=dst, send_sem=send, recv_sem=recv,
            device_id=device, device_id_type=MESH,
        ).start()

    def wait(ref, sem):
        pltpu.make_async_copy(ref, ref, sem).wait()

    consts = [(table_in, table), (merid_in, merid), (merid_t_in, merid_t), (spec_in, spec)]
    for i, (src, dst) in enumerate(consts):
        pltpu.make_async_copy(src, dst, csem.at[i]).start()

    barrier = pltpu.get_barrier_semaphore()
    for s in range(1, n_lon):
        pl.semaphore_signal(barrier, 1, device_id=at_lon(my_lon ^ s), device_id_type=MESH)
    for s in range(1, n_lat):
        pl.semaphore_signal(barrier, 1, device_id=at_lat(my_lat ^ s), device_id_type=MESH)
    mem_peer = (1 - my_mem, my_lat, my_lon)
    pl.semaphore_signal(barrier, 1, device_id=mem_peer, device_id_type=MESH)
    pl.semaphore_wait(barrier, n_lon + n_lat - 1)

    def send_strips(c):
        lv, b = split(c)
        dst = xin.at[lv, my_lon, :, cells(b)]

        def each(lon, go):
            @pl.when(lon < n_lon - 1)
            def _():
                go(ctrl.at[lv, pl.ds(aligned(lon * GROUP, GROUP), GROUP), cells(b)])

            @pl.when(lon == n_lon - 1)
            def _():
                go(ctrl_last.at[lv, :, cells(b)])

        for s in lon_order:
            lon = my_lon ^ s
            each(lon, lambda src, lon=lon: remote(src, dst, xs.at[c], xr.at[c], at_lon(lon)))
        each(my_lon, lambda src: pltpu.make_async_copy(src, dst, xr.at[c]).start())

    def load_perturbs(c):
        lv, b = split(c)
        slot = lax.rem(c, 2)
        for e in range(n_lon - 1):
            pltpu.make_async_copy(
                pert.at[lv, pl.ds(e * GROUP, GROUP), cells(b)], pbuf.at[slot, e], ps.at[slot]
            ).start()
        pltpu.make_async_copy(
            pert_last.at[lv, :, cells(b)], pbuf.at[slot, n_lon - 1], ps.at[slot]
        ).start()

    for c in range(min(AHEAD, chunks)):
        send_strips(c)
    load_perturbs(0)
    for i, (src, dst) in enumerate(consts):
        pltpu.make_async_copy(src, dst, csem.at[i]).wait()

    low = lax.broadcasted_iota(jnp.int32, (step, LANES), 1) < HALF
    low_16 = low.astype(F32).astype(BF16)
    high_16 = (1.0 - low.astype(F32)).astype(BF16)

    def forward(c):
        lv, b = split(c)
        wait(xin.at[lv, :, :, cells(b)], xr.at[c])

        def two_rows(i, carry):
            for e in range(n_lon):
                at = pl.ds(aligned(b * width + i * (2 * cols), LANES), 2 * cols)
                x = xin[lv, e, :, at].astype(F32)
                x = jnp.concatenate([x[:, :cols], x[:, cols:]], 0).astype(BF16)
                rows_in[pl.ds(aligned(i * 16, 16), 16), e * cols : (e + 1) * cols] = x
            return carry

        lax.fori_loop(0, step // 2, two_rows, 0)
        for k in range(0, waves.shape[0], 2):
            at = slice(k * LANES, (k + 2) * LANES)
            pair_k = jnp.dot(rows_in[...], table[:, at], preferred_element_type=F32)
            waves[k] = pair_k[:, :LANES]
            waves[k + 1] = pair_k[:, LANES:]
        for p in range(pairs):
            for d in range(n_lat):
                main = d
                in_a = rest_a // LANES + d // 2
                in_b = rest_b // LANES + d // 2
                first, second = (in_a, in_b) if d % 2 == 0 else (in_b, in_a)
                even, odd = pl.ds(2 * p, step, GROUP), pl.ds(2 * p + 1, step, GROUP)
                last = jnp.where(low, waves[first, even, :], waves[second, odd, :])
                at = p * pair
                wst[lv, d, band(b), at : at + LANES] = waves[main, even, :].astype(BF16)
                wst[lv, d, band(b), at + LANES : at + 2 * LANES] = waves[main, odd, :].astype(BF16)
                wst[lv, d, band(b), at + 2 * LANES : at + pair] = last.astype(BF16)
        dst = zin.at[lv, my_lat, band(b), :]
        for s in lat_order:
            lat = my_lat ^ s
            remote(wst.at[lv, lat, band(b), :], dst, zs.at[c], zr.at[c], at_lat(lat))
        pltpu.make_async_copy(wst.at[lv, my_lat, band(b), :], dst, zr.at[c]).start()

    def spectral(lv):
        def arrived(b, carry):
            wait(zin.at[lv, :, band(b), :], zr.at[lv * blocks + b])
            return carry

        lax.fori_loop(0, blocks, arrived, 0)
        for p in range(pairs):
            at = slice(p * pair, (p + 1) * pair)
            columns = zin[lv, :, :, at].reshape(n_lat * rows, pair)
            coef = jnp.dot(merid_t[...], columns, preferred_element_type=F32)
            kind = 1 if p == pairs - 1 else 0
            scaled[:, at] = (coef * spec[kind]).astype(BF16)

    def backward(c):
        lv, b = split(c)
        lhs = jnp.concatenate([merid[d, band(b), :] for d in range(n_lat)], 0)
        for p in range(pairs):
            at = slice(p * pair, (p + 1) * pair)
            back = jnp.dot(lhs, scaled[:, at], preferred_element_type=F32).astype(BF16)
            for d in range(n_lat):
                zin[lv, d, band(b), at] = back[d * step : (d + 1) * step]
        dst = bin_.at[lv, my_lat, band(b), :]
        for s in lat_order:
            lat = my_lat ^ s
            remote(zin.at[lv, lat, band(b), :], dst, bs.at[c], br.at[c], at_lat(lat))
        pltpu.make_async_copy(zin.at[lv, my_lat, band(b), :], dst, br.at[c]).start()

    def to_grid(c):
        lv, b = split(c)
        wait(bin_.at[lv, :, band(b), :], br.at[c])
        for p in range(pairs):
            even = slice(2 * p * step, (2 * p + 1) * step)
            odd = slice((2 * p + 1) * step, (2 * p + 2) * step)
            at = p * pair
            for s in range(n_lat):
                main = slice(s * LANES, (s + 1) * LANES)
                in_a = slice(rest_a + s // 2 * LANES, rest_a + (s // 2 + 1) * LANES)
                in_b = slice(rest_b + s // 2 * LANES, rest_b + (s // 2 + 1) * LANES)
                first, second = (in_a, in_b) if s % 2 == 0 else (in_b, in_a)
                rest = bin_[lv, s, band(b), at + 2 * LANES : at + pair]
                rows_out[even, main] = bin_[lv, s, band(b), at : at + LANES]
                rows_out[odd, main] = bin_[lv, s, band(b), at + LANES : at + 2 * LANES]
                rows_out[even, first] = rest * low_16
                rows_out[odd, second] = rest * high_16
        for e in range(n_lon):
            part_e = lax.dot_general(
                rows_out[...], table[e * cols : (e + 1) * cols, :],
                (((1,), (1,)), ((), ())), preferred_element_type=F32,
            )
            for m in range(GROUP):
                for j in range(cols // LANES):
                    tile = part_e[m * step : (m + 1) * step, j * LANES : (j + 1) * LANES]
                    grid[e % 2, j, pl.ds(m, step, GROUP), :] = tile

            def two_rows(i, carry):
                x = [
                    grid[e % 2, j, pl.ds(aligned(i * 16 + h, GROUP), GROUP), :]
                    for h in (0, GROUP)
                    for j in range(cols // LANES)
                ]
                x = jnp.concatenate(x, 1).astype(BF16)
                at = pl.ds(aligned(b * width + i * (2 * cols), LANES), 2 * cols)
                xin[lv, e, :, at] = x
                return carry

            lax.fori_loop(0, step // 2, two_rows, 0)
        dst = gin.at[lv, my_lon, :, cells(b)]
        for s in lon_order:
            lon = my_lon ^ s
            remote(xin.at[lv, lon, :, cells(b)], dst, gs.at[c], gr.at[c], at_lon(lon))
        pltpu.make_async_copy(xin.at[lv, my_lon, :, cells(b)], dst, gr.at[c]).start()

    owns = jnp.where(my_mem == 0, 1.0, 0.0).astype(F32)
    is_static = lax.broadcasted_iota(jnp.int32, (GROUP, cols), 0) == GROUP - 1

    def gather_sum(c):
        lv, b = split(c)
        slot = lax.rem(c, 2)
        wait(pbuf.at[slot], ps.at[slot])

        @pl.when(c + 1 < chunks)
        def _():
            load_perturbs(c + 1)

        wait(gin.at[lv, :, :, cells(b)], gr.at[c])
        w = weight[lv]

        def eight_rows(i, carry):
            sums = []
            for y in range(GROUP):
                off = aligned(i * (GROUP * cols) + y * cols, LANES)
                total = jnp.zeros((GROUP, cols), F32)
                for e in range(n_lon):
                    at = pl.ds(aligned(b * width + off, LANES), cols)
                    field = gin[lv, e, :, at].astype(F32)
                    factor = pbuf[slot, e, :, pl.ds(off, cols)].astype(F32) * (1.0 - w)
                    if e == n_lon - 1:
                        factor = jnp.where(is_static, owns * w, factor)
                    total += field * factor
                sums.append(jnp.sum(total, 0, keepdims=True))
            at = pl.ds(aligned(lv * rows + b * step + i * GROUP, GROUP), GROUP)
            part[at, :] = jnp.concatenate(sums, 0)
            return carry

        lax.fori_loop(0, step // GROUP, eight_rows, 0)
        at = pl.ds(aligned(lv * rows + b * step, GROUP), step)
        remote(part.at[at, :], peer.at[at, :], ms.at[c], mr.at[c], mem_peer)

    def finish(c):
        at = pl.ds(aligned(c * step, GROUP), step)
        wait(peer.at[at, :], mr.at[c])
        out[at, :] = part[at, :] + peer[at, :]

    lag_back = blocks + 1
    lag_grid = lag_back + 2
    lag_sum = lag_grid + 2
    lag_end = lag_sum + 1

    def one_step(t, carry):
        @pl.when(t + AHEAD < chunks)
        def _():
            send_strips(t + AHEAD)

        @pl.when(t < chunks)
        def _():
            forward(t)

        @pl.when((lax.rem(t, blocks) == 1 % blocks) & (t > blocks) & (t < lag_back + chunks))
        def _():
            spectral(lax.div(t - 1, blocks) - 1)

        @pl.when((t >= lag_back) & (t < lag_back + chunks))
        def _():
            backward(t - lag_back)

        @pl.when((t >= lag_grid) & (t < lag_grid + chunks))
        def _():
            to_grid(t - lag_grid)

        @pl.when((t >= lag_sum) & (t < lag_sum + chunks))
        def _():
            gather_sum(t - lag_sum)

        @pl.when((t >= lag_end) & (t < lag_end + chunks))
        def _():
            finish(t - lag_end)

        return carry

    lax.fori_loop(0, chunks + lag_end, one_step, 0)

    def drain(c, carry):
        lv, b = split(c)
        wait(xin.at[lv, : n_lon - 1, :, cells(b)], xs.at[c])
        wait(wst.at[lv, : n_lat - 1, band(b), :], zs.at[c])
        wait(zin.at[lv, : n_lat - 1, band(b), :], bs.at[c])
        wait(xin.at[lv, : n_lon - 1, :, cells(b)], gs.at[c])
        wait(part.at[pl.ds(aligned(c * step, GROUP), step), :], ms.at[c])
        return carry

    lax.fori_loop(0, chunks, drain, 0)


def in_one_kernel(
    control, perturbs, static_input, lat_basis, local_spectrum, static_spectrum, static_weight
):
    mem_dev, levels = control.shape[:2]
    cells = control.shape[-1]
    n_lat, n_lon = lax.axis_size("lat"), lax.axis_size("lon")
    rows = NLAT // n_lat
    cols = cells // rows
    step = STEP_ROWS
    klat = lat_basis.shape[1]
    chunks = levels * rows // step
    plain = lambda a: jnp.moveaxis(a.reshape(mem_dev, levels, cells), 0, 1)
    ctrl, pert = plain(control), plain(perturbs)
    tail = mem_dev + 1 - GROUP
    ctrl_last = jnp.concatenate([ctrl[:, tail:], static_input.reshape(levels, 1, cells)], 1)
    pert_last = jnp.pad(pert[:, tail:], ((0, 0), (0, 1), (0, 0)))

    def pair_of(even, odd):
        return jnp.concatenate(
            [even[:, :LANES], odd[:, :LANES], even[:, LANES:], odd[:, LANES:]], 1
        )

    own = jnp.where(lax.axis_index("lon") == n_lon - 1, static_spectrum, local_spectrum)
    spec = jnp.stack([pair_of(local_spectrum, local_spectrum), pair_of(local_spectrum, own)])
    table = jnp.asarray(packed_table(n_lat))
    sizes = (levels, n_lat, n_lon, rows, cols, step)
    pair = 3 * LANES
    packed = GROUP // 2 * pair
    sems = lambda n: pltpu.SemaphoreType.DMA((n,))
    hbm = pl.BlockSpec(memory_space=pl.ANY)
    result = pl.pallas_call(
        functools.partial(kernel, sizes),
        out_shape=jax.ShapeDtypeStruct((levels * rows, cols), F32),
        in_specs=[hbm] * 8 + [pl.BlockSpec(memory_space=pltpu.SMEM)],
        out_specs=pl.BlockSpec(memory_space=pltpu.VMEM),
        scratch_shapes=[
            pltpu.VMEM((levels, n_lon, GROUP, cells), BF16),
            pltpu.VMEM((levels, n_lat, rows, packed), BF16),
            pltpu.VMEM((levels, n_lat, rows, packed), BF16),
            pltpu.VMEM((levels, n_lat, rows, packed), BF16),
            pltpu.VMEM((levels, n_lon, GROUP, cells), BF16),
            pltpu.VMEM(table.shape, BF16),
            pltpu.VMEM((n_lat, rows, klat), BF16),
            pltpu.VMEM((klat, NLAT), BF16),
            pltpu.VMEM(spec.shape, F32),
            pltpu.VMEM((klat, packed), BF16),
            pltpu.VMEM((step * GROUP, NLON), BF16),
            pltpu.VMEM((table.shape[1] // LANES, step * GROUP, LANES), F32),
            pltpu.VMEM((step * GROUP, table.shape[1]), BF16),
            pltpu.VMEM((2, cols // LANES, step * GROUP, LANES), F32),
            pltpu.VMEM((2, n_lon, GROUP, step * cols), BF16),
            pltpu.VMEM((levels * rows, cols), F32),
            pltpu.VMEM((levels * rows, cols), F32),
            sems(4),
            *[sems(chunks)] * 10,
            sems(2),
        ],
        compiler_params=pltpu.CompilerParams(
            collective_id=0, has_side_effects=True, vmem_limit_bytes=67043328
        ),
        name="covariance",
    )(
        ctrl, ctrl_last, pert, pert_last, table,
        lat_basis.reshape(n_lat, rows, klat), lat_basis.T, spec, static_weight,
    )
    return result.reshape(levels, 1, 1, cells)


def mul(spec, a, b):
    return jnp.einsum(spec, a, b, preferred_element_type=jnp.float32)


def by_waves(
    control, perturbs, static_input, lat_basis, local_spectrum, static_spectrum, static_weight
):
    mem_dev, levels = (control.shape[0], control.shape[1])
    cell_count = control.shape[-1]
    lat_rows = NLAT // lax.axis_size("lat")
    lon_cols = cell_count // lat_rows
    fields = jnp.concatenate([control, static_input[None]], 0).reshape(-1, lat_rows, lon_cols)
    per_lon = fields.shape[0] // lax.axis_size("lon")
    field_index = lax.axis_index("lon") * per_lon + jnp.arange(per_lon, dtype=jnp.int32)
    is_static = field_index >= mem_dev * levels
    first_mem = (lax.axis_index("mem") == 0).astype(jnp.float32)
    zonal = jnp.asarray(zonal_table())
    strips = lax.all_to_all(fields, "lon", split_axis=0, concat_axis=2, tiled=True)
    waves = mul("bxn,nk->kbx", strips, zonal).astype(jnp.bfloat16)
    merid = lax.all_to_all(waves, "lat", split_axis=0, concat_axis=2, tiled=True)
    coef = mul("kby,yj->kbj", merid, lat_basis)
    spectrum = jnp.where(
        is_static[None, :, None], static_spectrum.T[:, None, :], local_spectrum.T[:, None, :]
    )
    scaled = (coef * spectrum).astype(jnp.bfloat16)
    back = mul("kbj,yj->kby", scaled, lat_basis).astype(jnp.bfloat16)
    zonal_rows = lax.all_to_all(back, "lat", split_axis=2, concat_axis=0, tiled=True)
    grid = mul("kbx,nk->bxn", zonal_rows, zonal).astype(jnp.bfloat16)
    pert_fields = perturbs.reshape(mem_dev, levels, lat_rows, lon_cols)
    weight = static_weight[:, None, None]
    filtered = lax.all_to_all(grid, "lon", split_axis=2, concat_axis=0, tiled=True).reshape(
        mem_dev + 1, levels, lat_rows, lon_cols
    )
    ensemble = mul("mlxn,mlxn->lxn", pert_fields, filtered[:mem_dev])
    static_part = filtered[mem_dev].astype(jnp.float32)
    own = first_mem * weight * static_part + (1.0 - weight) * ensemble
    total = lax.psum(own, "mem")
    return total.reshape(levels, 1, 1, cell_count)


def fits(control):
    n_mem, n_lat, n_lon = (lax.axis_size(a) for a in ("mem", "lat", "lon"))
    rows = NLAT // n_lat
    cols = control.shape[-1] // rows
    return (
        n_mem == 2
        and control.shape[0] + 1 == GROUP * n_lon
        and KLON // n_lat == LANES + HALF
        and n_lat & (n_lat - 1) == 0
        and n_lon & (n_lon - 1) == 0
        and rows % STEP_ROWS == 0
        and cols % LANES == 0
        and rows // STEP_ROWS > 1
    )


def solution(mesh):
    def shards(control, *rest):
        body = in_one_kernel if fits(control) else by_waves
        return body(control, *rest)

    return jax.shard_map(
        shards,
        mesh=mesh,
        in_specs=(
            P("mem", None, "lat", "lon", None),
            P("mem", None, "lat", "lon", None),
            P(None, "lat", "lon", None),
            P(),
            P(None, "lat"),
            P(None, "lat"),
            P(),
        ),
        out_specs=P(None, "lat", "lon", None),
        check_vma=False,
    )
```

profile of v0, /device:TPU:18, one launch (start us, length us, event | category | flops | bytes accessed | tf_op | source)
XLA Modules:
  0.0 365.0 jit_solution(10389614275387363335)
XLA Ops:
  0.0 1.8 copy.16
  1.8 2.2 slice.29
  4.1 3.5 pad_maximum_fusion.ctrl_last
  7.5 2.2 slice.30
  9.8 0.0 copy-start
  9.8 0.0 copy-start.1
  9.8 0.0 copy-start.2
  9.8 2.4 pad.4.pert_last
  12.2 0.0 copy-done
  12.2 1.1 copy.17
  13.3 0.0 copy-done.1
  13.3 0.2 copy.18
  13.5 0.0 copy-done.2
  13.5 0.2 copy.21
  13.7 0.1 broadcast_select_fusion
  13.8 0.2 fusion.1
  13.9 1.1 pad_maximum_fusion.1.spec_in
  15.0 346.6 %covariance.1 = f32[576,384]{1,0:T(8,128)} custom-call(bf16[3,31,73728]{2,1,0:T(8,128)(2,1)} %bitcast.14, bf16[3,8,73728]{2,1,0:T(8,128)(2,1)} %pad_maximum_fusion.ctrl_last, bf16[3,31,73728]{2,1,0:T(8,128)(2,1)} %bitcast.16, bf16[3,8,73728]{2,1,0:T(8,128)(2,1)} %pad.4.pert_last, bf16[1536,1024]{1,0:T(8,128)(2,1)} %constant.11.clone.table_in, ...), custom_call_target="tpu_custom_call" | custom-call | tf_op jit(solution)/shard_map/covariance/pallas_call | solution.py:369
  361.7 3.3 reshape.20
  (4 shorter events, 0.1 us)
Async XLA Ops:
  9.8 2.4 copy-start
  9.8 3.5 copy-start.1
  9.8 3.7 %copy-start.2 = (f32[384,192]{0,1:T(8,128)S(1)}, f32[384,192]{0,1:T(8,128)}, u32[]{:S(2)}) copy-start(f32[384,192]{0,1:T(8,128)} %param.13) | copy-start | bytes 884740
where the time goes:
time: 370 us; the launch traced here: 365 us
  Pallas kernels  347 us (94%)
  local copies, waits for them, and re-layouts  13.5 us (4%)
  other arithmetic  4.79 us (1%)
    pallas_call x1, Pallas kernels, in_one_kernel(): pl.pallas_call(functools.partial(kernel, sizes), out_shape=jax.ShapeDtype...  347 us

commit v1 on v0

--- a/solution.py
+++ b/solution.py
@@ -14,7 +14,7 @@
 LANES = 128
 HALF = 64
 GROUP = 8
-STEP_ROWS = 32
+STEP_ROWS = 16
 AHEAD = 4
 MESH = pl.DeviceIdType.MESH
 F32, BF16 = jnp.float32, jnp.bfloat16
@@ -43,11 +43,11 @@
 
 def kernel(
     sizes,
-    ctrl, ctrl_last, pert, pert_last, table_in, merid_in, merid_t_in, spec_in, weight,
+    ctrl, pert, static_in, table_in, merid_in, local_in, global_in, weight,
     out,
     xin, wst, zin, bin_, gin, table, merid, merid_t, spec,
-    scaled, rows_in, waves, rows_out, grid, pbuf, part, peer,
-    csem, xs, xr, zs, zr, bs, br, gs, gr, ms, mr, ps,
+    scaled, rows_in, waves, rows_out, grid, cbuf, pbuf, static, local_t, global_t, part, peer,
+    csem, xs, xr, zs, zr, bs, br, gs, gr, ms, mr, cs, ps,
 ):
     levels, n_lat, n_lon, rows, cols, step = sizes
     blocks = rows // step
@@ -85,7 +85,11 @@
     def wait(ref, sem):
         pltpu.make_async_copy(ref, ref, sem).wait()
 
-    consts = [(table_in, table), (merid_in, merid), (merid_t_in, merid_t), (spec_in, spec)]
+    tail = (n_lon - 1) * GROUP
+    consts = [
+        (static_in, static), (merid_in, merid), (local_in, local_t), (global_in, global_t),
+        (table_in, table),
+    ]
     for i, (src, dst) in enumerate(consts):
         pltpu.make_async_copy(src, dst, csem.at[i]).start()
 
@@ -98,40 +102,70 @@
     pl.semaphore_signal(barrier, 1, device_id=mem_peer, device_id_type=MESH)
     pl.semaphore_wait(barrier, n_lon + n_lat - 1)
 
+    def load_members(src, buf, sem, c):
+        lv, b = split(c)
+        slot = lax.rem(c, 2)
+        return pltpu.make_async_copy(src.at[lv, :, cells(b)], buf.at[slot], sem.at[slot])
+
     def send_strips(c):
         lv, b = split(c)
         dst = xin.at[lv, my_lon, :, cells(b)]
-
-        def each(lon, go):
-            @pl.when(lon < n_lon - 1)
-            def _():
-                go(ctrl.at[lv, pl.ds(aligned(lon * GROUP, GROUP), GROUP), cells(b)])
-
-            @pl.when(lon == n_lon - 1)
-            def _():
-                go(ctrl_last.at[lv, :, cells(b)])
+        stage = gin.at[lv, my_lon, :, cells(b)]
+
+        def strip(lon):
+            return ctrl.at[lv, pl.ds(aligned(lon * GROUP, GROUP), GROUP), cells(b)]
+
+        def send(src, lon):
+            remote(src, dst, xs.at[c], xr.at[c], at_lon(lon))
 
         for s in lon_order:
             lon = my_lon ^ s
-            each(lon, lambda src, lon=lon: remote(src, dst, xs.at[c], xr.at[c], at_lon(lon)))
-        each(my_lon, lambda src: pltpu.make_async_copy(src, dst, xr.at[c]).start())
-
-    def load_perturbs(c):
-        lv, b = split(c)
-        slot = lax.rem(c, 2)
-        for e in range(n_lon - 1):
-            pltpu.make_async_copy(
-                pert.at[lv, pl.ds(e * GROUP, GROUP), cells(b)], pbuf.at[slot, e], ps.at[slot]
-            ).start()
-        pltpu.make_async_copy(
-            pert_last.at[lv, :, cells(b)], pbuf.at[slot, n_lon - 1], ps.at[slot]
-        ).start()
-
+
+            @pl.when(lon < n_lon - 1)
+            def _(lon=lon):
+                send(strip(lon), lon)
+
+        load_members(ctrl, cbuf, cs, c).wait()
+
+        @pl.when(c + 1 < chunks)
+        def _():
+            load_members(ctrl, cbuf, cs, c + 1).start()
+
+        def two_rows(i, carry):
+            at = pl.ds(aligned(i * (2 * cols), LANES), 2 * cols)
+            all_at = pl.ds(aligned(b * width + i * (2 * cols), LANES), 2 * cols)
+            x = cbuf[lax.rem(c, 2), tail:, at].astype(F32)
+            v = static[:, all_at].astype(F32)
+            row = v[levels - 1 : levels]
+            for k in range(levels - 1):
+                row = jnp.where(lv == k, v[k : k + 1], row)
+            gin[lv, my_lon, :, all_at] = jnp.concatenate([x, row], 0).astype(BF16)
+            return carry
+
+        lax.fori_loop(0, step // 2, two_rows, 0)
+
+        @pl.when(my_lon < n_lon - 1)
+        def _():
+            send(stage, n_lon - 1)
+            pltpu.make_async_copy(strip(my_lon), dst, xr.at[c]).start()
+
+        @pl.when(my_lon == n_lon - 1)
+        def _():
+            pltpu.make_async_copy(stage, dst, xr.at[c]).start()
+
+    load_members(ctrl, cbuf, cs, 0).start()
+    load_members(pert, pbuf, ps, 0).start()
+    pltpu.make_async_copy(static_in, static, csem.at[0]).wait()
     for c in range(min(AHEAD, chunks)):
         send_strips(c)
-    load_perturbs(0)
-    for i, (src, dst) in enumerate(consts):
-        pltpu.make_async_copy(src, dst, csem.at[i]).wait()
+    for i, (src, dst) in enumerate(consts[1:]):
+        pltpu.make_async_copy(src, dst, csem.at[i + 1]).wait()
+    for d in range(n_lat):
+        merid_t[d] = merid[d].astype(F32).T.astype(BF16)
+    shared = jnp.where(my_lon == n_lon - 1, global_t[...], local_t[...])
+    for kind, (even, odd) in enumerate([(local_t[...], local_t[...]), (local_t[...], shared)]):
+        both = jnp.concatenate([even[:LANES], odd[:LANES], even[LANES:], odd[LANES:]], 0)
+        spec[kind] = both.T
 
     low = lax.broadcasted_iota(jnp.int32, (step, LANES), 1) < HALF
     low_16 = low.astype(F32).astype(BF16)
@@ -181,8 +215,10 @@
         lax.fori_loop(0, blocks, arrived, 0)
         for p in range(pairs):
             at = slice(p * pair, (p + 1) * pair)
-            columns = zin[lv, :, :, at].reshape(n_lat * rows, pair)
-            coef = jnp.dot(merid_t[...], columns, preferred_element_type=F32)
+            coef = sum(
+                jnp.dot(merid_t[d], zin[lv, d, :, at], preferred_element_type=F32)
+                for d in range(n_lat)
+            )
             kind = 1 if p == pairs - 1 else 0
             scaled[:, at] = (coef * spec[kind]).astype(BF16)
 
@@ -240,22 +276,22 @@
 
             lax.fori_loop(0, step // 2, two_rows, 0)
         dst = gin.at[lv, my_lon, :, cells(b)]
+        wait(xin.at[lv, : n_lon - 1, :, cells(b)], xs.at[c])
         for s in lon_order:
             lon = my_lon ^ s
             remote(xin.at[lv, lon, :, cells(b)], dst, gs.at[c], gr.at[c], at_lon(lon))
         pltpu.make_async_copy(xin.at[lv, my_lon, :, cells(b)], dst, gr.at[c]).start()
 
     owns = jnp.where(my_mem == 0, 1.0, 0.0).astype(F32)
-    is_static = lax.broadcasted_iota(jnp.int32, (GROUP, cols), 0) == GROUP - 1
 
     def gather_sum(c):
         lv, b = split(c)
         slot = lax.rem(c, 2)
-        wait(pbuf.at[slot], ps.at[slot])
+        load_members(pert, pbuf, ps, c).wait()
 
         @pl.when(c + 1 < chunks)
         def _():
-            load_perturbs(c + 1)
+            load_members(pert, pbuf, ps, c + 1).start()
 
         wait(gin.at[lv, :, :, cells(b)], gr.at[c])
         w = weight[lv]
@@ -265,14 +301,16 @@
             for y in range(GROUP):
                 off = aligned(i * (GROUP * cols) + y * cols, LANES)
                 total = jnp.zeros((GROUP, cols), F32)
-                for e in range(n_lon):
-                    at = pl.ds(aligned(b * width + off, LANES), cols)
-                    field = gin[lv, e, :, at].astype(F32)
-                    factor = pbuf[slot, e, :, pl.ds(off, cols)].astype(F32) * (1.0 - w)
-                    if e == n_lon - 1:
-                        factor = jnp.where(is_static, owns * w, factor)
-                    total += field * factor
-                sums.append(jnp.sum(total, 0, keepdims=True))
+                here = pl.ds(off, cols)
+                there = pl.ds(aligned(b * width + off, LANES), cols)
+                for e in range(n_lon - 1):
+                    factor = pbuf[slot, e * GROUP : (e + 1) * GROUP, here].astype(F32)
+                    total += gin[lv, e, :, there].astype(F32) * factor
+                field = gin[lv, n_lon - 1, :, there].astype(F32)
+                last = field[: GROUP - 1] * pbuf[slot, tail:, here].astype(F32)
+                total = (1.0 - w) * (jnp.sum(total, 0, keepdims=True) + jnp.sum(last, 0, keepdims=True))
+                total += owns * w * field[GROUP - 1 :]
+                sums.append(total)
             at = pl.ds(aligned(lv * rows + b * step + i * GROUP, GROUP), GROUP)
             part[at, :] = jnp.concatenate(sums, 0)
             return carry
@@ -284,7 +322,11 @@
     def finish(c):
         at = pl.ds(aligned(c * step, GROUP), step)
         wait(peer.at[at, :], mr.at[c])
-        out[at, :] = part[at, :] + peer[at, :]
+        both = part[at, :] + peer[at, :]
+        lv, b = split(c)
+        for y in range(step):
+            there = pl.ds(aligned(b * width + y * cols, LANES), cols)
+            out[pl.ds(lv, 1), there] = both[y : y + 1]
 
     lag_back = blocks + 1
     lag_grid = lag_back + 2
@@ -326,7 +368,6 @@
 
     def drain(c, carry):
         lv, b = split(c)
-        wait(xin.at[lv, : n_lon - 1, :, cells(b)], xs.at[c])
         wait(wst.at[lv, : n_lat - 1, band(b), :], zs.at[c])
         wait(zin.at[lv, : n_lat - 1, band(b), :], bs.at[c])
         wait(xin.at[lv, : n_lon - 1, :, cells(b)], gs.at[c])
@@ -349,17 +390,6 @@
     chunks = levels * rows // step
     plain = lambda a: jnp.moveaxis(a.reshape(mem_dev, levels, cells), 0, 1)
     ctrl, pert = plain(control), plain(perturbs)
-    tail = mem_dev + 1 - GROUP
-    ctrl_last = jnp.concatenate([ctrl[:, tail:], static_input.reshape(levels, 1, cells)], 1)
-    pert_last = jnp.pad(pert[:, tail:], ((0, 0), (0, 1), (0, 0)))
-
-    def pair_of(even, odd):
-        return jnp.concatenate(
-            [even[:, :LANES], odd[:, :LANES], even[:, LANES:], odd[:, LANES:]], 1
-        )
-
-    own = jnp.where(lax.axis_index("lon") == n_lon - 1, static_spectrum, local_spectrum)
-    spec = jnp.stack([pair_of(local_spectrum, local_spectrum), pair_of(local_spectrum, own)])
     table = jnp.asarray(packed_table(n_lat))
     sizes = (levels, n_lat, n_lon, rows, cols, step)
     pair = 3 * LANES
@@ -368,8 +398,8 @@
     hbm = pl.BlockSpec(memory_space=pl.ANY)
     result = pl.pallas_call(
         functools.partial(kernel, sizes),
-        out_shape=jax.ShapeDtypeStruct((levels * rows, cols), F32),
-        in_specs=[hbm] * 8 + [pl.BlockSpec(memory_space=pltpu.SMEM)],
+        out_shape=jax.ShapeDtypeStruct((levels, cells), F32),
+        in_specs=[hbm] * 7 + [pl.BlockSpec(memory_space=pltpu.SMEM)],
         out_specs=pl.BlockSpec(memory_space=pltpu.VMEM),
         scratch_shapes=[
             pltpu.VMEM((levels, n_lon, GROUP, cells), BF16),
@@ -379,18 +409,23 @@
             pltpu.VMEM((levels, n_lon, GROUP, cells), BF16),
             pltpu.VMEM(table.shape, BF16),
             pltpu.VMEM((n_lat, rows, klat), BF16),
-            pltpu.VMEM((klat, NLAT), BF16),
-            pltpu.VMEM(spec.shape, F32),
+            pltpu.VMEM((n_lat, klat, rows), BF16),
+            pltpu.VMEM((2, klat, pair), F32),
             pltpu.VMEM((klat, packed), BF16),
             pltpu.VMEM((step * GROUP, NLON), BF16),
             pltpu.VMEM((table.shape[1] // LANES, step * GROUP, LANES), F32),
             pltpu.VMEM((step * GROUP, table.shape[1]), BF16),
             pltpu.VMEM((2, cols // LANES, step * GROUP, LANES), F32),
-            pltpu.VMEM((2, n_lon, GROUP, step * cols), BF16),
+            pltpu.VMEM((2, mem_dev, step * cols), BF16),
+            pltpu.VMEM((2, mem_dev, step * cols), BF16),
+            pltpu.VMEM((levels, cells), BF16),
+            pltpu.VMEM(local_spectrum.shape[::-1], F32),
+            pltpu.VMEM(local_spectrum.shape[::-1], F32),
             pltpu.VMEM((levels * rows, cols), F32),
             pltpu.VMEM((levels * rows, cols), F32),
-            sems(4),
+            sems(5),
             *[sems(chunks)] * 10,
+            sems(2),
             sems(2),
         ],
         compiler_params=pltpu.CompilerParams(
@@ -398,8 +433,8 @@
         ),
         name="covariance",
     )(
-        ctrl, ctrl_last, pert, pert_last, table,
-        lat_basis.reshape(n_lat, rows, klat), lat_basis.T, spec, static_weight,
+        ctrl, pert, static_input.reshape(levels, cells), table,
+        lat_basis.reshape(n_lat, rows, klat), local_spectrum.T, static_spectrum.T, static_weight,
     )
     return result.reshape(levels, 1, 1, cells)
 

time: 370 us -> 339 us (0.916); the launches traced: 365 us -> 339 us
  Pallas kernels: 347 us -> 336 us
  local copies, waits for them, and re-layouts: 13.5 us -> 3.09 us
  other arithmetic: 4.79 us -> 0 us
    pallas_call x1, Pallas kernels: 347 us -> 336 us  [in_one_kernel(): pl.pallas_call(functools.partial(kernel, sizes), out_shape=jax.ShapeDtype...]
    slice x6 -> x0, local copies, waits for them, and re-layouts: 4.52 us -> none  [the longest x1 2.23 us: in_one_kernel(): ctrl[:, tail:]]
where the time goes in v1:
time: 339 us
  Pallas kernels  336 us (99%)
    pallas_call x1, Pallas kernels, in_one_kernel(): pl.pallas_call(functools.partial(kernel, sizes), out_shape=jax.ShapeDtype...  336 us

profile of v1, /device:TPU:18, one launch (start us, length us, event | category | flops | bytes accessed | tf_op | source)
XLA Modules:
  0.0 339.0 jit_solution(8239482621815801731)
XLA Ops:
  0.0 335.9 %covariance.1 = f32[3,73728]{1,0:T(4,128)} custom-call(bf16[3,31,73728]{2,1,0:T(8,128)(2,1)} %bitcast.11, bf16[3,31,73728]{2,1,0:T(8,128)(2,1)} %bitcast.12, bf16[3,73728]{1,0:T(4,128)(2,1)} %bitcast.14, bf16[1536,1024]{1,0:T(8,128)(2,1)} %constant.2.clone.table_in, bf16[4,192,384]{2,1,0:T(8,128)(2,1)} %bitcast.15, f32[192,384]{1,0:T(8,128)} %bitcast.16, ...), custom_call_target="tpu_custom_call" | custom-call | tf_op jit(solution)/shard_map/covariance/pallas_call | solution.py:399
  335.9 3.1 copy.9

commit v2 on v1

--- a/solution.py
+++ b/solution.py
@@ -175,15 +175,12 @@
         lv, b = split(c)
         wait(xin.at[lv, :, :, cells(b)], xr.at[c])
 
-        def two_rows(i, carry):
+        for i in range(step // 2):
             for e in range(n_lon):
                 at = pl.ds(aligned(b * width + i * (2 * cols), LANES), 2 * cols)
                 x = xin[lv, e, :, at].astype(F32)
                 x = jnp.concatenate([x[:, :cols], x[:, cols:]], 0).astype(BF16)
-                rows_in[pl.ds(aligned(i * 16, 16), 16), e * cols : (e + 1) * cols] = x
-            return carry
-
-        lax.fori_loop(0, step // 2, two_rows, 0)
+                rows_in[i * 16 : (i + 1) * 16, e * cols : (e + 1) * cols] = x
         for k in range(0, waves.shape[0], 2):
             at = slice(k * LANES, (k + 2) * LANES)
             pair_k = jnp.dot(rows_in[...], table[:, at], preferred_element_type=F32)
@@ -253,34 +250,31 @@
                 rows_out[odd, main] = bin_[lv, s, band(b), at + LANES : at + 2 * LANES]
                 rows_out[even, first] = rest * low_16
                 rows_out[odd, second] = rest * high_16
-        for e in range(n_lon):
+        wait(xin.at[lv, : n_lon - 1, :, cells(b)], xs.at[c])
+        dst = gin.at[lv, my_lon, :, cells(b)]
+        for turn, s in enumerate(lon_order + [0]):
+            lon = my_lon ^ s
+            strip = table[pl.ds(aligned(lon * cols, LANES), cols), :]
             part_e = lax.dot_general(
-                rows_out[...], table[e * cols : (e + 1) * cols, :],
-                (((1,), (1,)), ((), ())), preferred_element_type=F32,
+                rows_out[...], strip, (((1,), (1,)), ((), ())), preferred_element_type=F32
             )
             for m in range(GROUP):
                 for j in range(cols // LANES):
                     tile = part_e[m * step : (m + 1) * step, j * LANES : (j + 1) * LANES]
-                    grid[e % 2, j, pl.ds(m, step, GROUP), :] = tile
-
-            def two_rows(i, carry):
+                    grid[turn % 2, j, pl.ds(m, step, GROUP), :] = tile
+            for i in range(step // 2):
                 x = [
-                    grid[e % 2, j, pl.ds(aligned(i * 16 + h, GROUP), GROUP), :]
+                    grid[turn % 2, j, i * 16 + h : i * 16 + h + GROUP, :]
                     for h in (0, GROUP)
                     for j in range(cols // LANES)
                 ]
-                x = jnp.concatenate(x, 1).astype(BF16)
                 at = pl.ds(aligned(b * width + i * (2 * cols), LANES), 2 * cols)
-                xin[lv, e, :, at] = x
-                return carry
-
-            lax.fori_loop(0, step // 2, two_rows, 0)
-        dst = gin.at[lv, my_lon, :, cells(b)]
-        wait(xin.at[lv, : n_lon - 1, :, cells(b)], xs.at[c])
-        for s in lon_order:
-            lon = my_lon ^ s
-            remote(xin.at[lv, lon, :, cells(b)], dst, gs.at[c], gr.at[c], at_lon(lon))
-        pltpu.make_async_copy(xin.at[lv, my_lon, :, cells(b)], dst, gr.at[c]).start()
+                xin[lv, lon, :, at] = jnp.concatenate(x, 1).astype(BF16)
+            src = xin.at[lv, lon, :, cells(b)]
+            if s:
+                remote(src, dst, gs.at[c], gr.at[c], at_lon(lon))
+            else:
+                pltpu.make_async_copy(src, dst, gr.at[c]).start()
 
     owns = jnp.where(my_mem == 0, 1.0, 0.0).astype(F32)
 
@@ -326,7 +320,7 @@
         lv, b = split(c)
         for y in range(step):
             there = pl.ds(aligned(b * width + y * cols, LANES), cols)
-            out[pl.ds(lv, 1), there] = both[y : y + 1]
+            out[lv, :, there] = both[y : y + 1]
 
     lag_back = blocks + 1
     lag_grid = lag_back + 2
@@ -398,7 +392,7 @@
     hbm = pl.BlockSpec(memory_space=pl.ANY)
     result = pl.pallas_call(
         functools.partial(kernel, sizes),
-        out_shape=jax.ShapeDtypeStruct((levels, cells), F32),
+        out_shape=jax.ShapeDtypeStruct((levels, 1, cells), F32),
         in_specs=[hbm] * 7 + [pl.BlockSpec(memory_space=pltpu.SMEM)],
         out_specs=pl.BlockSpec(memory_space=pltpu.VMEM),
         scratch_shapes=[

time: 339 us -> 336 us (level)
  no operation moved by 1% of the time
where the time goes in v2:
time: 336 us
  Pallas kernels  334 us (99%)
    pallas_call x1, Pallas kernels, in_one_kernel(): pl.pallas_call(functools.partial(kernel, sizes), out_shape=jax.ShapeDtype...  334 us

profile of v2, /device:TPU:18, one launch (start us, length us, event | category | flops | bytes accessed | tf_op | source)
XLA Modules:
  0.0 335.8 jit_solution(9268343618221296419)
XLA Ops:
  0.0 333.6 %covariance.1 = f32[3,1,73728]{2,1,0:T(1,128)} custom-call(bf16[3,31,73728]{2,1,0:T(8,128)(2,1)} %bitcast.13, bf16[3,31,73728]{2,1,0:T(8,128)(2,1)} %bitcast.14, bf16[3,73728]{1,0:T(4,128)(2,1)} %bitcast.16, bf16[1536,1024]{1,0:T(8,128)(2,1)} %constant.2.clone.table_in, bf16[4,192,384]{2,1,0:T(8,128)(2,1)} %bitcast.17, f32[192,384]{1,0:T(8,128)} %bitcast.18, ...), custom_call_target="tpu_custom_call" | custom-call | tf_op jit(solution)/shard_map/covariance/pallas_call | solution.py:393
  333.6 2.1 copy.11

commit v3 on v2

--- a/solution.py
+++ b/solution.py
@@ -44,9 +44,9 @@
 def kernel(
     sizes,
     ctrl, pert, static_in, table_in, merid_in, local_in, global_in, weight,
-    out,
+    part, peer,
     xin, wst, zin, bin_, gin, table, merid, merid_t, spec,
-    scaled, rows_in, waves, rows_out, grid, cbuf, pbuf, static, local_t, global_t, part, peer,
+    scaled, rows_in, waves, rows_out, grid, cbuf, pbuf, static, local_t, global_t,
     csem, xs, xr, zs, zr, bs, br, gs, gr, ms, mr, cs, ps,
 ):
     levels, n_lat, n_lon, rows, cols, step = sizes
@@ -291,7 +291,6 @@
         w = weight[lv]
 
         def eight_rows(i, carry):
-            sums = []
             for y in range(GROUP):
                 off = aligned(i * (GROUP * cols) + y * cols, LANES)
                 total = jnp.zeros((GROUP, cols), F32)
@@ -304,23 +303,15 @@
                 last = field[: GROUP - 1] * pbuf[slot, tail:, here].astype(F32)
                 total = (1.0 - w) * (jnp.sum(total, 0, keepdims=True) + jnp.sum(last, 0, keepdims=True))
                 total += owns * w * field[GROUP - 1 :]
-                sums.append(total)
-            at = pl.ds(aligned(lv * rows + b * step + i * GROUP, GROUP), GROUP)
-            part[at, :] = jnp.concatenate(sums, 0)
+                part[lv, :, there] = total
             return carry
 
         lax.fori_loop(0, step // GROUP, eight_rows, 0)
-        at = pl.ds(aligned(lv * rows + b * step, GROUP), step)
-        remote(part.at[at, :], peer.at[at, :], ms.at[c], mr.at[c], mem_peer)
+        remote(part.at[lv, :, cells(b)], peer.at[lv, :, cells(b)], ms.at[c], mr.at[c], mem_peer)
 
     def finish(c):
-        at = pl.ds(aligned(c * step, GROUP), step)
-        wait(peer.at[at, :], mr.at[c])
-        both = part[at, :] + peer[at, :]
-        lv, b = split(c)
-        for y in range(step):
-            there = pl.ds(aligned(b * width + y * cols, LANES), cols)
-            out[lv, :, there] = both[y : y + 1]
+        lv, b = split(c)
+        wait(peer.at[lv, :, cells(b)], mr.at[c])
 
     lag_back = blocks + 1
     lag_grid = lag_back + 2
@@ -365,7 +356,7 @@
         wait(wst.at[lv, : n_lat - 1, band(b), :], zs.at[c])
         wait(zin.at[lv, : n_lat - 1, band(b), :], bs.at[c])
         wait(xin.at[lv, : n_lon - 1, :, cells(b)], gs.at[c])
-        wait(part.at[pl.ds(aligned(c * step, GROUP), step), :], ms.at[c])
+        wait(part.at[lv, :, cells(b)], ms.at[c])
         return carry
 
     lax.fori_loop(0, chunks, drain, 0)
@@ -390,11 +381,11 @@
     packed = GROUP // 2 * pair
     sems = lambda n: pltpu.SemaphoreType.DMA((n,))
     hbm = pl.BlockSpec(memory_space=pl.ANY)
-    result = pl.pallas_call(
+    own, other = pl.pallas_call(
         functools.partial(kernel, sizes),
-        out_shape=jax.ShapeDtypeStruct((levels, 1, cells), F32),
+        out_shape=[jax.ShapeDtypeStruct((levels, 1, cells), F32)] * 2,
         in_specs=[hbm] * 7 + [pl.BlockSpec(memory_space=pltpu.SMEM)],
-        out_specs=pl.BlockSpec(memory_space=pltpu.VMEM),
+        out_specs=[pl.BlockSpec(memory_space=pltpu.VMEM)] * 2,
         scratch_shapes=[
             pltpu.VMEM((levels, n_lon, GROUP, cells), BF16),
             pltpu.VMEM((levels, n_lat, rows, packed), BF16),
@@ -415,8 +406,6 @@
             pltpu.VMEM((levels, cells), BF16),
             pltpu.VMEM(local_spectrum.shape[::-1], F32),
             pltpu.VMEM(local_spectrum.shape[::-1], F32),
-            pltpu.VMEM((levels * rows, cols), F32),
-            pltpu.VMEM((levels * rows, cols), F32),
             sems(5),
             *[sems(chunks)] * 10,
             sems(2),
@@ -430,7 +419,7 @@
         ctrl, pert, static_input.reshape(levels, cells), table,
         lat_basis.reshape(n_lat, rows, klat), local_spectrum.T, static_spectrum.T, static_weight,
     )
-    return result.reshape(levels, 1, 1, cells)
+    return (own + other).reshape(levels, 1, 1, cells)
 
 
 def mul(spec, a, b):

time: 336 us -> 338 us (level)
  no operation moved by 1% of the time
where the time goes in v3:
time: 338 us
  Pallas kernels  335 us (99%)
    pallas_call x1, Pallas kernels, in_one_kernel(): pl.pallas_call(functools.partial(kernel, sizes), out_shape=[jax.ShapeDtyp...  335 us

profile of v3, /device:TPU:18, one launch (start us, length us, event | category | flops | bytes accessed | tf_op | source)
XLA Modules:
  0.0 337.9 jit_solution(1974080653804803038)
XLA Ops:
  0.0 334.6 %covariance.1 = (f32[3,1,73728]{2,1,0:T(1,128)}, f32[3,1,73728]{2,1,0:T(1,128)}) custom-call(bf16[3,31,73728]{2,1,0:T(8,128)(2,1)} %bitcast.14, bf16[3,31,73728]{2,1,0:T(8,128)(2,1)} %bitcast.15, bf16[3,73728]{1,0:T(4,128)(2,1)} %bitcast.16, bf16[1536,1024]{1,0:T(8,128)(2,1)} %constant.2.clone.table_in, bf16[4,192,384]{2,1,0:T(8,128)(2,1)} %bitcast.17, ...), custom_call_target="tpu_custom_call" | custom-call | tf_op jit(solution)/shard_map/covariance/pallas_call | solution.py:384
  334.6 3.3 add_bitcast_fusion
